TPU v7x, 32 devices: a whole 2x2x4 slice. The times are simulated.
32 devices in a mesh: dp: 4 (over y, core), seq: 8 (over z, x).
Axes of the slice: x: 2, y: 2, z: 4, core: 2. Of those that a mesh axis runs over, the one named last changes fastest.
Arguments:
- tokens: bfloat16 [32768, 2048], P(('dp', 'seq')), parts along dimension 0, may hold values from -6 to 6
- chosen: int32 [4096], P('dp'), parts along dimension 0, may hold values from 0 to 8191, as said below
- gates: float32 [4096], P('dp'), parts along dimension 0, may hold values from 0.5 to 2
- w_query: bfloat16 [2048, 1024], P('seq'), may hold values from -1.8561553 to 1.8561553
- w_key: bfloat16 [2048, 256], P('seq'), may hold values from -0.088388348 to 0.088388348
- w_value: bfloat16 [2048, 256], P('seq'), may hold values from -0.125 to 0.125
- w_out: bfloat16 [1024, 2048], P(None, 'seq'), may hold values from -0.5 to 0.5
Outputs:
- mixed: bfloat16 [32768, 2048], P(('dp', 'seq')), parts along dimension 0
There are 4 independent parts, one for each index of `dp`. A program takes and returns all parts, laid end to end along the dimension named above; an argument that names none is the same for every part. Nothing has to cross between parts.
Inputs may be any that keep to these rules, and one draw needn't show every extreme that they name: `chosen`: distinct positions in increasing order; at most 256 of them lie in one device's 1024 consecutive positions, and exactly 256 lie in some device's positions.
All inputs are finite; a program needn't handle non-finite values.
Results may differ from a plain program's by a relative error of at most 0.006.
Values may be sent and summed in bfloat16 or wider, within the bound.
A program may use at most 128 MiB of HBM per device.

v0:
```python
import math

import jax
import jax.numpy as jnp
from jax import lax
from jax.sharding import PartitionSpec as P

HEADS = 8
KV_HEADS = 2
HEAD_DIM = 128
ROWS_DEV = 128
MOST_OWN = 256


neg_fill = -1e30


def normalize(row_block):
    widened = row_block.astype(jnp.float32)
    scale_rows = lax.rsqrt(jnp.mean(widened * widened, axis=1, keepdims=True) + 1e-06)
    return (widened * scale_rows).astype(jnp.bfloat16)


def per_device(tokens, chosen, gates, w_query, w_key, w_value, w_out):
    shards = lax.axis_size("seq")
    my_index = lax.axis_index("seq")
    tok_rows = tokens.shape[0]
    model_width = tokens.shape[1]
    picked_total = chosen.shape[0]
    slot_count = (MOST_OWN - 1) // shards + 1
    group_size = HEADS // KV_HEADS
    owner_of = chosen // tok_rows
    owners = jnp.arange(shards, dtype=jnp.int32)
    counts = jnp.sum((owner_of[None, :] == owners[:, None]).astype(jnp.int32), axis=1)
    starts = jnp.cumsum(counts) - counts
    my_start = starts[my_index]
    my_count = counts[my_index]
    my_base = my_index * tok_rows
    own_steps = jnp.arange(MOST_OWN, dtype=jnp.int32)
    own_valid = own_steps < my_count
    slot_steps = jnp.arange(slot_count, dtype=jnp.int32)
    lead_step = (owners - my_start) % shards
    offset = lead_step[:, None] + shards * slot_steps[None, :]
    is_valid = offset < my_count
    flat_ids = jnp.clip((my_start + offset).reshape(-1), 0, picked_total - 1)
    flat_valid = is_valid.reshape(-1)
    spot_row = jnp.where(flat_valid, chosen[flat_ids] - my_base, 0)
    row_block = normalize(tokens[spot_row])
    outgoing = jnp.where(flat_valid[:, None], row_block, jnp.zeros_like(row_block)).reshape(
        shards, slot_count, model_width
    )
    arrived = lax.all_to_all(outgoing, "seq", split_axis=0, concat_axis=0, tiled=True)
    local_rows = jnp.arange(ROWS_DEV, dtype=jnp.int32)
    query_order = my_index + shards * local_rows
    source = owner_of[query_order]
    place_at = source * slot_count + (query_order - starts[source]) // shards
    normed = arrived.reshape(shards * slot_count, model_width)[place_at]

    def key_order_of(row_ids):
        return row_ids // ROWS_DEV + shards * (row_ids % ROWS_DEV)

    rows_here = normed.shape[0]
    pieces = (
        lax.all_gather(w_query, "seq", axis=0, tiled=True),
        lax.all_gather(w_key, "seq", axis=0, tiled=True),
        lax.all_gather(w_value, "seq", axis=0, tiled=True),
    )
    query_sum, key_sum, value_sum = tuple(
        (jnp.dot(normed, piece_now, preferred_element_type=jnp.float32) for piece_now in pieces)
    )
    query_matrix = (
        (query_sum * HEAD_DIM ** (-0.5))
        .astype(jnp.bfloat16)
        .reshape(rows_here, KV_HEADS, group_size, HEAD_DIM)
    )
    keys_all = key_sum.astype(jnp.bfloat16)
    values = value_sum.astype(jnp.bfloat16)
    start_state = (
        jnp.full((KV_HEADS, group_size, rows_here), neg_fill, jnp.float32),
        jnp.zeros((KV_HEADS, group_size, rows_here), jnp.float32),
        jnp.zeros((KV_HEADS, group_size, rows_here, HEAD_DIM), jnp.float32),
    )
    key_rows = lax.all_gather(keys_all, "seq", axis=0, tiled=True)
    value_rows = lax.all_gather(values, "seq", axis=0, tiled=True)
    length = key_rows.shape[0]
    block_rows = math.gcd(length, 512)

    def one_block(step_no, inner_state):
        top_score, weight, mixed_sum = inner_state
        first_row = step_no * block_rows
        key_portion = lax.dynamic_slice_in_dim(key_rows, first_row, block_rows, 0).reshape(
            block_rows, KV_HEADS, HEAD_DIM
        )
        value_piece = lax.dynamic_slice_in_dim(value_rows, first_row, block_rows, 0).reshape(
            block_rows, KV_HEADS, HEAD_DIM
        )
        key_order = key_order_of(first_row + jnp.arange(block_rows, dtype=jnp.int32))
        logit_scores = jnp.einsum(
            "qjfh,ujh->jfqu", query_matrix, key_portion, preferred_element_type=jnp.float32
        )
        allowed = key_order[None, :] <= query_order[:, None]
        logit_scores = jnp.where(allowed, logit_scores, neg_fill)
        fresh_top = jnp.maximum(top_score, jnp.max(logit_scores, axis=-1))
        weights_now = jnp.where(allowed, jnp.exp(logit_scores - fresh_top[..., None]), 0.0)
        shrink = jnp.exp(top_score - fresh_top)
        weight = weight * shrink + jnp.sum(weights_now, axis=-1)
        mixed_sum = mixed_sum * shrink[..., None] + jnp.einsum(
            "yoih,hyf->yoif",
            weights_now.astype(jnp.bfloat16),
            value_piece,
            preferred_element_type=jnp.float32,
        )
        return (fresh_top, weight, mixed_sum)

    top_score, weight, mixed_sum = lax.fori_loop(0, length // block_rows, one_block, start_state)
    attended = (
        jnp.transpose(mixed_sum / weight[..., None], (2, 0, 1, 3))
        .reshape(rows_here, HEADS * HEAD_DIM)
        .astype(jnp.bfloat16)
    )
    block_out = jnp.dot(
        attended,
        lax.all_gather(w_out, "seq", axis=1, tiled=True),
        preferred_element_type=jnp.float32,
    ).astype(jnp.bfloat16)
    own_compact = jnp.clip(my_start + own_steps, 0, picked_total - 1)
    slot_steps = jnp.arange(slot_count, dtype=jnp.int32)
    lead_back = (my_index - starts) % shards
    offset_back = lead_back[:, None] + shards * slot_steps[None, :]
    valid_back = offset_back < counts[:, None]
    local_k = jnp.clip((starts[:, None] + offset_back - my_index) // shards, 0, ROWS_DEV - 1)
    outgoing_back = jnp.where(
        valid_back[..., None], block_out[local_k], jnp.zeros((), jnp.bfloat16)
    )
    returned = lax.all_to_all(outgoing_back, "seq", split_axis=0, concat_axis=0, tiled=True)
    pick_at = (my_start + own_steps) % shards * slot_count + jnp.clip(
        own_steps // shards, 0, slot_count - 1
    )
    delta_rows = returned.reshape(shards * slot_count, model_width)[pick_at]
    spot_row = jnp.where(own_valid, chosen[own_compact] - my_base, tok_rows)
    lift_rows = gates[own_compact][:, None] * delta_rows.astype(jnp.float32)
    mixed = tokens.astype(jnp.float32).at[spot_row].add(lift_rows, mode="drop")
    return mixed.astype(jnp.bfloat16)


def solution(mesh):
    return jax.shard_map(
        per_device,
        mesh=mesh,
        in_specs=(
            P(("dp", "seq"), None),
            P("dp"),
            P("dp"),
            P("seq", None),
            P("seq", None),
            P("seq", None),
            P(None, "seq"),
        ),
        out_specs=P(("dp", "seq"), None),
        check_vma=False,
    )
```

profile of v0, /device:TPU:28, one launch (start us, length us, event | category | flops | bytes accessed | tf_op | source)
XLA Modules:
  0.0 314.4 jit_solution(3164678104505626016)
XLA Ops:
  6.5 0.7 all-gather.9.cloned.1.call-update
  7.3 0.7 all-gather.5.cloned.1.call-update
  9.3 0.7 add_select_fusion.3
  13.8 1.4 gather_fusion.2
  15.3 5.1 %gather_fusion.3 = bf16[256,2048]{1,0:T(8,128)(2,1)S(1)} fusion(bf16[1024,2048]{1,0:T(8,128)(2,1)} %param.9, s32[1024]{0:T(1024)S(1)} %pad_clamp_fusion.4), kind=kCustom, calls=%fused_computation.3 | custom fusion | bytes 2098176 | tf_op jit(solution)/shard_map/gather | solution.py:48
  20.7 1.3 fusion.21
  22.0 6.0 %all-to-all-start = ((bf16[8,32,2048]{2,1,0:T(8,128)(2,1)}), bf16[8,32,2048]{2,1,0:T(8,128)(2,1)S(1)}, u32[]{:S(2)}, u32[]{:S(2)}) async-start(bf16[8,32,2048]{2,1,0:T(8,128)(2,1)} %fusion.21), calls=%async_computation | async-start | bytes 2097152 | tf_op jit(solution)/shard_map/all_to_all | solution.py:52
  28.1 1.0 gather_fusion.4
  29.2 4.9 %fusion.40 = s32[128]{0:T(128)S(1)} fusion(s32[128]{0:T(128)S(1)} %gather_fusion.4, s32[]{:T(128)} %bitcast.16, s32[]{:T(128)} %bitcast.17, s32[]{:T(128)} %bitcast.18, s32[]{:T(128)} %bitcast.19, s32[]{:T(128)} %bitcast.20, s32[]{:T(128)} %bitcast.22, s32[]{:T(128)} %bitcast.21, s32[]{:T(128)} %bitcast.15, s32[]{:T(128)} %axis_index.12), kind=kLoop, calls=%fused_computation.132 | loop fusion | flops 5120 | bytes 1060 | tf_op jit(solution)/shard_map/select_n | solution.py:57
  34.2 26.0 %all-to-all-done = bf16[8,32,2048]{2,1,0:T(8,128)(2,1)S(1)} async-done(((bf16[8,32,2048]{2,1,0:T(8,128)(2,1)}), bf16[8,32,2048]{2,1,0:T(8,128)(2,1)S(1)}, u32[]{:S(2)}, u32[]{:S(2)}) %all-to-all-start) | async-done | bytes 1048608 | tf_op jit(solution)/shard_map/all_to_all | solution.py:52
  60.2 0.9 gather_fusion.5
  61.2 1.5 convolution_convert_fusion.1
  62.7 31.0 %all_gather.22 = bf16[1024,256]{1,0:T(8,128)(2,1)S(1)} all-gather(bf16[128,256]{1,0:T(8,128)(2,1)S(1)} %convolution_convert_fusion.1), channel_id=1, replica_groups=mesh['dp'=4,'seq'=8] {'seq'}, dimensions={0}, use_global_device_ids=true | all-gather | bytes 589824 | tf_op jit(solution)/shard_map/all_gather | solution.py:84
  93.7 8.9 %all-gather.5.cloned.1.call-done = bf16[2048,256]{1,0:T(8,128)(2,1)} async-done(((bf16[256,256]{1,0:T(8,128)(2,1)}), bf16[2048,256]{1,0:T(8,128)(2,1)}) %all-gather.5.cloned.1.call-update) | async-done | bytes 1048592 | tf_op jit(solution)/shard_map/all_gather | solution.py:65
  102.6 1.5 convolution_convert_fusion.2
  104.1 31.4 %all_gather.19 = bf16[1024,256]{1,0:T(8,128)(2,1)S(1)} all-gather(bf16[128,256]{1,0:T(8,128)(2,1)S(1)} %convolution_convert_fusion.2), channel_id=1, replica_groups=mesh['dp'=4,'seq'=8] {'seq'}, dimensions={0}, use_global_device_ids=true | all-gather | bytes 589824 | tf_op jit(solution)/shard_map/all_gather | solution.py:83
  135.5 43.7 %all-gather.7.cloned.1.call-done = bf16[2048,1024]{1,0:T(8,128)(2,1)} async-done(((bf16[256,1024]{1,0:T(8,128)(2,1)}), bf16[2048,1024]{1,0:T(8,128)(2,1)}) %all-gather.7.cloned.1.call-update) | async-done | bytes 4194320 | tf_op jit(solution)/shard_map/all_gather | solution.py:64
  179.2 2.9 fusion.20
  182.3 4.9 %while.20 = (s32[]{:T(128)}, f32[2,4,128]{2,1,0:T(4,128)S(1)}, f32[2,4,128]{2,1,0:T(4,128)S(1)}, f32[2,4,128,128]{3,2,1,0:T(8,128)S(1)}, bf16[1024,256]{1,0:T(8,...) while((s32[]{:T(128)}, f32[2,4,128]{2,1,0:T(4,128)S(1)}, ...), condition=%wide.region_6.7_spmd.clone, body=%wide.region_3.6_spmd.clone.sunk | while | flops 274153728 | bytes 10556611 | solution.py:115
  183.9 0.9 convolution_add_fusion.2
  186.3 0.9 convolution_add_fusion.2
  187.5 66.3 %all-gather.11.cloned.1.call-done = bf16[1024,2048]{1,0:T(8,128)(2,1)} async-done(((bf16[1024,256]{1,0:T(8,128)(2,1)}), bf16[1024,2048]{1,0:T(8,128)(2,1)}) %all-gather.11.cloned.1.call-update) | async-done | bytes 4194320 | tf_op jit(solution)/shard_map/all_gather | solution.py:123
  253.9 2.9 convolution_convert_fusion
  256.8 1.4 gather_fusion.6
  258.2 1.1 broadcast_select_fusion
  259.3 5.9 %all-to-all-start.1 = ((bf16[8,32,2048]{2,1,0:T(8,128)(2,1)}), bf16[8,32,2048]{2,1,0:T(8,128)(2,1)S(1)}, u32[]{:S(2)}, u32[]{:S(2)}) async-start(bf16[8,32,2048]{2,1,0:T(8,128)(2,1)} %broadcast_select_fusion), calls=%async_computation.1 | async-start | bytes 2097152 | tf_op jit(solution)/shard_map/all_to_all | solution.py:135
  265.2 6.5 %convert_element_type.56 = f32[1024,2048]{1,0:T(8,128)} convert(bf16[1024,2048]{1,0:T(8,128)(2,1)} %param.9) | non-fusion elementwise | flops 2097152 | bytes 12582912 | tf_op jit(solution)/shard_map/convert_element_type | solution.py:142
  272.3 1.4 gather_fusion
  273.7 1.4 gather_fusion.1
  275.8 12.3 %all-to-all-done.1 = bf16[8,32,2048]{2,1,0:T(8,128)(2,1)S(1)} async-done(((bf16[8,32,2048]{2,1,0:T(8,128)(2,1)}), bf16[8,32,2048]{2,1,0:T(8,128)(2,1)S(1)}, u32[]{:S(2)}, u32[]{:S(2)}) %all-to-all-start.1) | async-done | bytes 1048608 | tf_op jit(solution)/shard_map/all_to_all | solution.py:135
  288.0 13.8 %scatter_custom_fusion = f32[1024,2048]{1,0:T(8,128)} fusion(f32[1024,2048]{1,0:T(8,128)} %convert_element_type.56, s32[256]{0:T(256)S(1)} %bitcast.130, f32[256]{0:T(256)S(1)} %gather_fusion.1, bf16[256,2048]{1,0:T(8,128)(2,1)S(1)} %bitcast.120, s32[1024]{0:T(1024)S(1)} %pad_clamp_fusion), kind=kCustom, calls=%fused_computation.43 | custom fusion | flops 1572864 | bytes 9442304 | tf_op jit(solution)/shard_map/scatter-add | solution.py:142
  301.8 6.0 %convert_element_type.70 = bf16[1024,2048]{1,0:T(8,128)(2,1)} convert(f32[1024,2048]{1,0:T(8,128)} %scatter_custom_fusion) | non-fusion elementwise | flops 2097152 | bytes 12582912 | tf_op jit(solution)/shard_map/convert_element_type | solution.py:143
  (70 shorter events, 10.4 us)
Async XLA Ops:
  6.5 267.2 %copy-start = (f32[1024]{0:T(1024)S(1)}, f32[1024]{0:T(1024)}, u32[]{:S(2)}) copy-start(f32[1024]{0:T(1024)} %param.11) | copy-start | bytes 12292
  6.5 7.3 %copy-start.1 = (s32[1024]{0:T(1024)S(1)}, s32[1024]{0:T(1024)}, u32[]{:S(2)}) copy-start(s32[1024]{0:T(1024)} %param.10) | copy-start | bytes 12292
  6.5 54.6 %all-gather.9.cloned.1.call-start = ((), (), s32[]{:S(2)}) async-start(), calls=%async_computation.4 | async-start | bytes 1179648 | tf_op jit(solution)/shard_map/all_gather | solution.py:66
  7.3 95.3 %all-gather.5.cloned.1.call-start = ((), (), s32[]{:S(2)}) async-start(), calls=%async_computation.2 | async-start | bytes 1179648 | tf_op jit(solution)/shard_map/all_gather | solution.py:65
  8.0 171.2 %all-gather.7.cloned.1.call-start = ((), (), s32[]{:S(2)}) async-start(), calls=%async_computation.3 | async-start | bytes 4718592 | tf_op jit(solution)/shard_map/all_gather | solution.py:64
  8.7 245.1 %all-gather.11.cloned.1.call-start = ((), (), s32[]{:S(2)}) async-start(), calls=%async_computation.5 | async-start | bytes 4718592 | tf_op jit(solution)/shard_map/all_gather | solution.py:123
  22.0 38.2 %all-to-all-start = ((bf16[8,32,2048]{2,1,0:T(8,128)(2,1)}), bf16[8,32,2048]{2,1,0:T(8,128)(2,1)S(1)}, u32[]{:S(2)}, u32[]{:S(2)}) async-start(bf16[8,32,2048]{2,1,0:T(8,128)(2,1)} %fusion.21), calls=%async_computation | async-start | bytes 2097152 | tf_op jit(solution)/shard_map/all_to_all | solution.py:52
  259.3 28.8 %all-to-all-start.1 = ((bf16[8,32,2048]{2,1,0:T(8,128)(2,1)}), bf16[8,32,2048]{2,1,0:T(8,128)(2,1)S(1)}, u32[]{:S(2)}, u32[]{:S(2)}) async-start(bf16[8,32,2048]{2,1,0:T(8,128)(2,1)} %broadcast_select_fusion), calls=%async_computation.1 | async-start | bytes 2097152 | tf_op jit(solution)/shard_map/all_to_all | solution.py:135
Sparse Core Ops, SparseCore 0:
  9.5 48.1 all-gather.8
  59.8 42.7 all-gather.4
  104.7 74.4 all-gather.6
  181.1 72.7 all-gather.10
where the time goes:
time: 319 us; the launch traced here: 314 us
  waiting for transfers between devices  160 us (50%)
  blocking collectives  62.4 us (20%)
  other arithmetic  39.7 us (12%)
  local copies, waits for them, and re-layouts  15.1 us (5%)
  between operations  13.4 us (4%)
  starting transfers between devices  12.1 us (4%)
  matrix products  11.8 us (4%)
    all_gather x1, waiting for transfers between devices, per_device(): lax.all_gather(w_out, 'seq', axis=1, tiled=True)  66.3 us
    all_gather x1, waiting for transfers between devices, per_device(): lax.all_gather(w_query, 'seq', axis=0, tiled=True)  43.7 us
    all_gather x1, blocking collectives, per_device(): key_rows = lax.all_gather(keys_all, 'seq', axis=0, tiled=True)  31.4 us
    all_gather x1, blocking collectives, per_device(): value_rows = lax.all_gather(values, 'seq', axis=0, tiled=True)  31 us
    all_to_all x1, waiting for transfers between devices, per_device(): lax.all_to_all(outgoing, 'seq', split_axis=0, concat_axis=0, tiled=True)  26 us
    scatter-add x1, other arithmetic, per_device(): mixed = tokens.astype(jnp.float32).at[spot_row].add(lift_rows, mode='drop')  13.8 us
    all_to_all x1, waiting for transfers between devices, per_device(): lax.all_to_all(outgoing_back, 'seq', split_axis=0, concat_axis=0, tiled=T...  12.3 us
    all_gather x1, waiting for transfers between devices, per_device(): lax.all_gather(w_key, 'seq', axis=0, tiled=True)  8.88 us
  transfers between devices with their start and end apart: 6, of which 5 were waited for; matrix products, arithmetic and copies ran while one was open for 13% of the time, Pallas kernels for 0%

commit v1 on v0

v1 whole, which is shorter than its diff:
```python
import functools

import jax
import jax.numpy as jnp
from jax import lax
from jax.experimental import pallas as pl
from jax.experimental.pallas import tpu as pltpu
from jax.sharding import PartitionSpec as P

HEADS = 8
KV_HEADS = 2
HEAD_DIM = 128
MOST_OWN = 256
MESH = pl.DeviceIdType.MESH
NEG = -1e30
F32 = jnp.float32
BF16 = jnp.bfloat16


class Ring:
    def __init__(self, geo, sems, region_in, region_y=None):
        self.g = geo
        self.sems = sems
        self.region_in = region_in
        self.region_y = region_y
        self.sends = []
        a_count, b_count = geo["A"], geo["B"]
        self.order = [(k, 0) for k in range(1, a_count)]
        self.order += [(k, j) for k in range(a_count) for j in range(1, b_count)]

    def piece(self, k, j):
        g = self.g
        a = lax.rem(g["a"] - k + g["A"], g["A"])
        b = lax.rem(g["b"] - j + g["B"], g["B"])
        return a * g["B"] + b

    def copy(self, kind, index, ref, dp, seq):
        send, recv = self.sems[kind]
        return pltpu.make_async_remote_copy(
            src_ref=ref,
            dst_ref=ref,
            send_sem=send.at[index],
            recv_sem=recv.at[index],
            device_id=(dp, seq),
            device_id_type=MESH,
        )

    def send(self, *args):
        made = self.copy(*args)
        made.start()
        self.sends.append(made)

    def arrive(self, kind, index, ref):
        self.copy(kind, index, ref, self.g["dp"], self.g["z_next"]).wait_recv()

    def mine(self, s):
        return self.region_in(s, self.g["y"], self.g["c"])

    def fan(self, k, j):
        if self.region_y is None:
            return
        g = self.g
        index = self.order.index((k, j))
        s = self.piece(k, j)
        self.send("y", index, self.region_y(s, g["y"], g["c"]), g["dp_y"], g["seq"])
        self.send("d", index, self.mine(s), g["dp_c"], g["seq"])

    def slow(self, k):
        g = self.g
        s = self.piece(k, 0)
        if k > 0:
            self.arrive("z", k - 1, self.mine(s))
        if k < g["A"] - 1:
            self.send("z", k, self.mine(s), g["dp"], g["z_next"])
        if g["B"] > 1:
            self.send("x", k * (g["B"] - 1), self.mine(s), g["dp"], g["x_next"])
        if k > 0:
            self.fan(k, 0)

    def fast(self, k, j):
        g = self.g
        s = self.piece(k, j)
        self.arrive("x", k * (g["B"] - 1) + j - 1, self.mine(s))
        if j < g["B"] - 1:
            self.send("x", k * (g["B"] - 1) + j, self.mine(s), g["dp"], g["x_next"])
        self.fan(k, j)

    def relay(self):
        g = self.g
        for index, (k, j) in enumerate(self.order):
            ref = self.region_y(self.piece(k, j), 1 - g["y"], g["c"])
            self.arrive("y", index, ref)
            self.send("d", len(self.order) + index, ref, g["dp_c"], g["seq"])

    def gather_core(self):
        g = self.g
        for index, (k, j) in enumerate(self.order):
            s = self.piece(k, j)
            self.arrive("d", index, self.region_in(s, g["y"], 1 - g["c"]))
            self.arrive("d", len(self.order) + index, self.region_y(s, 1 - g["y"], 1 - g["c"]))

    def finish(self):
        for made in self.sends:
            made.wait_send()


def main_kernel(
    A, B, tok, ch, wq, wk, wv, wo, blk, oh_out,
    tok_v, wbuf, obuf, kvbuf, normed, qs, acc, m_s, l_s, att, lsem,
    wz, wx, wy, wd, oz, ox, oy, od, kz, kx,
):
    n = A * B
    dp = lax.axis_index("dp")
    seq = lax.axis_index("seq")
    a, b = seq // B, lax.rem(seq, B)
    y, c = lax.rem(dp // 2, 2), lax.rem(dp, 2)
    z_next = lax.rem(a + 1, A) * B + b
    z_prev = lax.rem(a + A - 1, A) * B + b
    x_next = a * B + lax.rem(b + 1, B)
    x_prev = a * B + lax.rem(b + B - 1, B)
    dp_y = dp + 2 * (1 - 2 * y)
    dp_c = dp + 1 - 2 * c
    geo = dict(
        A=A, B=B, a=a, b=b, y=y, c=c, dp=dp, seq=seq,
        z_next=z_next, x_next=x_next, dp_y=dp_y, dp_c=dp_c,
    )
    t_rows = tok.shape[0]
    width = tok.shape[1]
    k_rows = wq.shape[0]
    q_cols, e_cols = wq.shape[1], wk.shape[1]
    all_cols = q_cols + 2 * e_cols
    o_rows, o_cols = wo.shape

    rows_here = pl.ds(pl.multiple_of(seq * k_rows, k_rows), k_rows)
    local = [
        (wq, wbuf.at[rows_here, pl.ds(0, q_cols)]),
        (wk, wbuf.at[rows_here, pl.ds(q_cols, e_cols)]),
        (wv, wbuf.at[rows_here, pl.ds(q_cols + e_cols, e_cols)]),
        (wo, obuf.at[seq]),
        (tok, tok_v),
    ]
    local = [pltpu.make_async_copy(s, d, lsem.at[i]) for i, (s, d) in enumerate(local)]
    for made in local:
        made.start()

    greet = [(dp, z_next)] + ([(dp, z_prev)] if A > 2 else [])
    if B > 1:
        greet += [(dp, x_next)] + ([(dp, x_prev)] if B > 2 else [])
    greet += [(dp_y, seq), (dp_c, seq)]
    barrier = pltpu.get_barrier_semaphore()
    for who in greet:
        pl.semaphore_signal(barrier, inc=1, device_id=who, device_id_type=MESH)
    pl.semaphore_wait(barrier, len(greet))

    third = all_cols // 6

    def w_region(s, start, size):
        return wbuf.at[
            pl.ds(pl.multiple_of(s * k_rows, k_rows), k_rows),
            pl.ds(pl.multiple_of(start, 128), size),
        ]

    o_half = o_rows // 2
    o_y = o_half * 3 // 8 // 16 * 16
    o_in = o_half - o_y

    def o_region(s, start, size):
        return obuf.at[s, pl.ds(pl.multiple_of(start, 16), size), :]

    ring_w = Ring(
        geo,
        {"z": wz, "x": wx, "y": wy, "d": wd},
        lambda s, y, c: w_region(s, c * (3 * third) + y * third, 2 * third),
        lambda s, y, c: w_region(s, c * (3 * third) + y * (2 * third), third),
    )
    ring_o = Ring(
        geo,
        {"z": oz, "x": ox, "y": oy, "d": od},
        lambda s, y, c: o_region(s, c * o_half + y * o_y, o_in),
        lambda s, y, c: o_region(s, c * o_half + y * o_in, o_y),
    )
    ring_k = Ring(geo, {"z": kz, "x": kx}, lambda s, y, c: kvbuf.at[s])

    for made in local[:3]:
        made.wait()
    ring_w.slow(0)

    base = seq * t_rows
    picks = ch[...]
    start = jnp.sum((picks < base).astype(F32), axis=1, keepdims=True)
    rel = picks - base
    inside = (rel >= 0) & (rel < t_rows)
    place = jnp.where(inside, (rel + 1).astype(F32), 0.0)
    order = lax.broadcasted_iota(jnp.int32, picks.shape, 1).astype(F32) - start
    slots = lax.broadcasted_iota(jnp.int32, (MOST_OWN, 1), 0).astype(F32)
    own = jnp.sum(jnp.where(order == slots, place, 0.0), axis=1, keepdims=True) - 1.0
    spots = lax.broadcasted_iota(jnp.int32, (1, t_rows), 1).astype(F32)
    oh_out[...] = (own == spots).astype(F32).astype(BF16)
    local[4].wait()
    chunk = 512
    square = jnp.zeros((MOST_OWN, 1), F32)
    for i in range(width // chunk):
        rows = jnp.dot(oh_out[...], tok_v[:, i * chunk : (i + 1) * chunk], preferred_element_type=F32)
        square = square + jnp.sum(rows * rows, axis=1, keepdims=True)
        normed[:, i * chunk : (i + 1) * chunk] = rows.astype(BF16)
    scale = lax.rsqrt(square / width + 1e-06)
    for i in range(width // chunk):
        cols = slice(i * chunk, (i + 1) * chunk)
        normed[:, cols] = (normed[:, cols].astype(F32) * scale).astype(BF16)

    for k in range(1, A):
        ring_w.slow(k)
        for j in range(1, B):
            ring_w.fast(k - 1, j)
    for j in range(1, B):
        ring_w.fast(A - 1, j)
    local[3].wait()
    ring_o.slow(0)
    ring_w.relay()
    ring_w.gather_core()

    kv_cols = 2 * e_cols
    for i in range(kv_cols // 256):
        part = jnp.dot(
            normed[...], wbuf[:, q_cols + i * 256 : q_cols + (i + 1) * 256], preferred_element_type=F32
        )
        kvbuf[seq, :, i * 256 : (i + 1) * 256] = part.astype(BF16)
    ring_k.slow(0)
    group = HEADS // KV_HEADS
    for i in range(q_cols // 256):
        part = jnp.dot(normed[...], wbuf[:, i * 256 : (i + 1) * 256], preferred_element_type=F32)
        part = (part * HEAD_DIM**-0.5).astype(BF16)
        for h in range(2):
            head = i * 2 + h
            first = (head % group) * MOST_OWN
            qs[head // group, first : first + MOST_OWN, :] = part[:, h * 128 : (h + 1) * 128]

    m_s[...] = jnp.full(m_s.shape, NEG, F32)
    l_s[...] = jnp.zeros(l_s.shape, F32)
    acc[...] = jnp.zeros(acc.shape, F32)

    def attend(t, diagonal):
        low = t * t_rows
        count = jnp.sum(
            ((picks >= low) & (picks < low + t_rows)).astype(F32), axis=1, keepdims=True
        )
        col = lax.broadcasted_iota(jnp.int32, (1, MOST_OWN), 1).astype(F32)
        allowed = col < count
        if diagonal:
            row = lax.broadcasted_iota(jnp.int32, (MOST_OWN, MOST_OWN), 0).astype(F32)
            allowed = jnp.logical_and(allowed, col <= row)

        def one(f, _):
            e = f // group
            first = pl.multiple_of(lax.rem(f, group) * MOST_OWN, MOST_OWN)
            rows = pl.ds(first, MOST_OWN)
            ecol = pl.multiple_of(e * HEAD_DIM, HEAD_DIM)
            keys = kvbuf[t, :, pl.ds(ecol, HEAD_DIM)]
            vals = kvbuf[t, :, pl.ds(e_cols + ecol, HEAD_DIM)]
            score = lax.dot_general(
                qs[e, rows, :], keys, (((1,), (1,)), ((), ())), preferred_element_type=F32
            )
            score = jnp.where(allowed, score, NEG)
            old = m_s[e, rows, :]
            top = jnp.maximum(old, jnp.max(score, axis=1, keepdims=True))
            prob = jnp.where(allowed, jnp.exp(score - top[:, :1]), 0.0)
            shrink = jnp.exp(old - top)
            m_s[e, rows, :] = top
            l_s[e, rows, :] = l_s[e, rows, :] * shrink + jnp.sum(prob, axis=1, keepdims=True)
            acc[e, rows, :] = acc[e, rows, :] * shrink + jnp.dot(
                prob.astype(BF16), vals, preferred_element_type=F32
            )
            return 0

        lax.fori_loop(0, HEADS, one, 0)

    def attend_past(t):
        @pl.when(t < seq)
        def _():
            attend(t, False)

    attend(seq, True)
    for k in range(1, A):
        ring_k.slow(k)
        ring_o.slow(k)
        for j in range(1, B):
            ring_k.fast(k - 1, j)
            ring_o.fast(k - 1, j)
        attend_past(ring_k.piece(k, 0))
        for j in range(1, B):
            attend_past(ring_k.piece(k - 1, j))
    for j in range(1, B):
        ring_o.fast(A - 1, j)
    ring_o.relay()
    for j in range(1, B):
        ring_k.fast(A - 1, j)
    for j in range(1, B):
        attend_past(ring_k.piece(A - 1, j))
    for head in range(HEADS):
        first = (head % group) * MOST_OWN
        rows = slice(first, first + MOST_OWN)
        total = l_s[head // group, rows, :]
        total = jnp.where(total > 0.0, total, 1.0)
        att[:, head * HEAD_DIM : (head + 1) * HEAD_DIM] = (
            acc[head // group, rows, :] / total
        ).astype(BF16)
    ring_o.gather_core()
    for s in range(n):
        blk[:, s * o_cols : (s + 1) * o_cols] = jnp.dot(
            att[...], obuf[s], preferred_element_type=F32
        ).astype(BF16)
    ring_w.finish()
    ring_k.finish()
    ring_o.finish()


def add_kernel(tile, tok, ch, gates, oh, blk, out):
    seq = lax.axis_index("seq")
    t_rows = tile * pl.num_programs(0)
    low = seq * t_rows + pl.program_id(0) * tile
    rows = lax.broadcasted_iota(jnp.int32, (tile, 1), 0) + low
    gate = jnp.sum(jnp.where(ch[...] == rows, gates[...], 0.0), axis=1, keepdims=True)
    lift = lax.dot_general(
        oh[...], blk[...], (((0,), (0,)), ((), ())), preferred_element_type=F32
    )
    out[...] = (tok[...].astype(F32) + gate * lift).astype(BF16)


def per_device(tokens, chosen, gates, w_query, w_key, w_value, w_out):
    n = lax.axis_size("seq")
    A = 4 if n % 4 == 0 else 1
    B = n // A
    t_rows, width = tokens.shape
    k_rows, q_cols = w_query.shape
    e_cols = w_key.shape[1]
    all_cols = q_cols + 2 * e_cols
    o_rows, o_cols = w_out.shape
    picks = chosen.reshape(1, -1)
    gate_row = gates.reshape(1, -1)
    dma = pltpu.SemaphoreType.DMA
    any_spec = pl.BlockSpec(memory_space=pl.ANY)
    vmem_spec = pl.BlockSpec(memory_space=pltpu.VMEM)
    steps_x = max(A * (B - 1), 1)

    def pair(count):
        return (dma((count,)), dma((count,)))

    sems = []
    for _ in range(2):
        sems += [pair(A - 1), pair(steps_x), pair(n - 1), pair(2 * (n - 1))]
    sems += [pair(A - 1), pair(steps_x)]
    flat = [x for two in sems for x in two]

    def body(*refs):
        head, tail = refs[: len(refs) - len(flat)], refs[len(refs) - len(flat) :]
        pairs = [(tail[i], tail[i + 1]) for i in range(0, len(tail), 2)]
        main_kernel(A, B, *head, *pairs)

    blk, oh = pl.pallas_call(
        body,
        out_shape=(
            jax.ShapeDtypeStruct((MOST_OWN, width), BF16),
            jax.ShapeDtypeStruct((MOST_OWN, t_rows), BF16),
        ),
        in_specs=[any_spec, vmem_spec] + [any_spec] * 4,
        out_specs=(vmem_spec, vmem_spec),
        scratch_shapes=[
            pltpu.VMEM((t_rows, width), BF16),
            pltpu.VMEM((n * k_rows, all_cols), BF16),
            pltpu.VMEM((n, o_rows, o_cols), BF16),
            pltpu.VMEM((n, MOST_OWN, 2 * e_cols), BF16),
            pltpu.VMEM((MOST_OWN, width), BF16),
            pltpu.VMEM((KV_HEADS, HEADS // KV_HEADS * MOST_OWN, HEAD_DIM), BF16),
            pltpu.VMEM((KV_HEADS, HEADS // KV_HEADS * MOST_OWN, HEAD_DIM), F32),
            pltpu.VMEM((KV_HEADS, HEADS // KV_HEADS * MOST_OWN, HEAD_DIM), F32),
            pltpu.VMEM((KV_HEADS, HEADS // KV_HEADS * MOST_OWN, HEAD_DIM), F32),
            pltpu.VMEM((MOST_OWN, HEADS * HEAD_DIM), BF16),
            dma((5,)),
            *flat,
        ],
        compiler_params=pltpu.CompilerParams(
            collective_id=0, has_side_effects=True, vmem_limit_bytes=60 * 1024 * 1024
        ),
        name="gather_attend",
    )(tokens, picks, w_query, w_key, w_value, w_out)

    tile = 128
    return pl.pallas_call(
        functools.partial(add_kernel, tile),
        grid=(t_rows // tile,),
        out_shape=jax.ShapeDtypeStruct((t_rows, width), BF16),
        in_specs=[
            pl.BlockSpec((tile, width), lambda i: (i, 0)),
            pl.BlockSpec(picks.shape, lambda i: (0, 0)),
            pl.BlockSpec(picks.shape, lambda i: (0, 0)),
            pl.BlockSpec((MOST_OWN, tile), lambda i: (0, i)),
            pl.BlockSpec((MOST_OWN, width), lambda i: (0, 0)),
        ],
        out_specs=pl.BlockSpec((tile, width), lambda i: (i, 0)),
        compiler_params=pltpu.CompilerParams(vmem_limit_bytes=32 * 1024 * 1024),
        name="add_rows",
    )(tokens, picks, gate_row, oh, blk)


def solution(mesh):
    return jax.shard_map(
        per_device,
        mesh=mesh,
        in_specs=(
            P(("dp", "seq"), None),
            P("dp"),
            P("dp"),
            P("seq", None),
            P("seq", None),
            P("seq", None),
            P(None, "seq"),
        ),
        out_specs=P(("dp", "seq"), None),
        check_vma=False,
    )
```

time: 319 us -> 96.3 us (0.30); the launches traced: 314 us -> 96 us
  waiting for transfers between devices: 160 us -> 0 us
  Pallas kernels: 0 us -> 91.5 us
  blocking collectives: 62.4 us -> 0 us
  other arithmetic: 39.7 us -> 0 us
  between operations: 13.4 us -> 0.04 us
  starting transfers between devices: 12.1 us -> 0 us
  matrix products: 11.8 us -> 0 us
  local copies, waits for them, and re-layouts: 15.1 us -> 4.46 us
    all_gather x4 -> x0, waiting for transfers between devices: 119 us -> none  [the longest x1 66.3 us: per_device(): lax.all_gather(w_out, 'seq', axis=1, tiled=True)]
    pallas_call x0 -> x2, Pallas kernels: none -> 91.5 us  [the longest x1 86.5 us: per_device(): pl.pallas_call(body, out_shape=(jax.ShapeDtypeStruct((MOST_OWN, width), B...]
    all_gather x2 -> x0, blocking collectives: 62.4 us -> none  [the longest x1 31.4 us: per_device(): key_rows = lax.all_gather(keys_all, 'seq', axis=0, tiled=True)]
    all_to_all x2 -> x0, waiting for transfers between devices: 38.3 us -> none  [the longest x1 26 us: per_device(): lax.all_to_all(outgoing, 'seq', split_axis=0, concat_axis=0, tiled=True)]
    scatter-add x1 -> x0, other arithmetic: 13.8 us -> none  [per_device(): mixed = tokens.astype(jnp.float32).at[spot_row].add(lift_rows, mode='drop')]
    gather x8 -> x0, local copies, waits for them, and re-layouts: 13.1 us -> none  [the longest x1 5.1 us: per_device(): row_block = normalize(tokens[spot_row])]
    convert_element_type x3 -> x0, other arithmetic: 12.6 us -> none  [the longest x1 6.49 us: per_device(): mixed = tokens.astype(jnp.float32).at[spot_row].add(lift_rows, mode='drop')]
    all_to_all x2 -> x0, starting transfers between devices: 12 us -> none  [the longest x1 6.03 us: per_device(): lax.all_to_all(outgoing, 'seq', split_axis=0, concat_axis=0, tiled=True)]
  transfers between devices with their start and end apart: 6 -> 0, of which waited for: 5 -> 0; matrix products, arithmetic and copies ran while one was open for 13% -> 0% of each run, Pallas kernels for 0% -> 0%
where the time goes in v1:
time: 96.3 us; the launch traced here: 96 us
  Pallas kernels  91.5 us (95%)
  local copies, waits for them, and re-layouts  4.46 us (5%)
    pallas_call x1, Pallas kernels, per_device(): pl.pallas_call(body, out_shape=(jax.ShapeDtypeStruct((MOST_OWN, width), B...  86.5 us
    pallas_call x1, Pallas kernels, per_device(): pl.pallas_call(functools.partial(add_kernel, tile), grid=(t_rows // tile,...  5.01 us
    unnamed x10, local copies, waits for them, and re-layouts  4.46 us

profile of v1, /device:TPU:28, one launch (start us, length us, event | category | flops | bytes accessed | tf_op | source)
XLA Modules:
  0.0 96.0 jit_solution(18015303040107501377)
XLA Ops:
  0.0 0.0 copy-start.4
  0.0 0.0 copy-start.3
  0.0 86.5 %gather_attend.1 = (bf16[256,2048]{1,0:T(8,128)(2,1)}, bf16[256,1024]{1,0:T(8,128)(2,1)}) custom-call(bf16[1024,2048]{1,0:T(8,128)(2,1)} %tok.1, s32[1,1024]{1,0:T(1,128)} %bitcast.2, bf16[256,1024]{1,0:T(8,128)(2,1)} %refs_2_.1, bf16[256,256]{1,0:T(8,128)(2,1)} %refs_3_.1, bf16[256,256]{1,0:T(8,128)(2,1)} %refs_4_.1, bf16[1024,256]{1,0:T(8,128)(2,1)} %refs_5_.1), custom_call_target="tpu_custom_call" | custom-call | tf_op jit(solution)/shard_map/gather_attend/pallas_call | solution.py:359
  86.5 0.0 copy-done.4
  86.5 0.0 copy-done.3
  86.5 0.0 copy-start
  86.6 2.2 %copy-done = bf16[1024,2048]{1,0:T(8,128)(2,1)S(1)} copy-done((bf16[1024,2048]{1,0:T(8,128)(2,1)S(1)}, bf16[1024,2048]{1,0:T(8,128)(2,1)}, u32[]{:S(2)}) %copy-start) | copy-done | bytes 4194328
  88.7 0.0 copy-start.1
  88.7 1.2 %copy-done.1 = bf16[256,2048]{1,0:T(8,128)(2,1)S(1)} copy-done((bf16[256,2048]{1,0:T(8,128)(2,1)S(1)}, bf16[256,2048]{1,0:T(8,128)(2,1)}, u32[]{:S(2)}) %copy-start.1) | copy-done | bytes 1048600
  90.0 0.0 copy-start.2
  90.0 1.0 %copy-done.2 = bf16[256,1024]{1,0:T(8,128)(2,1)S(1)} copy-done((bf16[256,1024]{1,0:T(8,128)(2,1)S(1)}, bf16[256,1024]{1,0:T(8,128)(2,1)}, u32[]{:S(2)}) %copy-start.2) | copy-done | bytes 524312
  91.0 5.0 %add_rows.1 = bf16[1024,2048]{1,0:T(8,128)(2,1)} custom-call(bf16[1024,2048]{1,0:T(8,128)(2,1)S(1)} %copy-done, s32[1,1024]{1,0:T(1,128)S(1)} %bitcast.3, f32[1,1024]{1,0:T(1,128)S(1)} %bitcast.4, bf16[256,1024]{1,0:T(8,128)(2,1)S(1)} %copy-done.2, bf16[256,2048]{1,0:T(8,128)(2,1)S(1)} %copy-done.1), custom_call_target="tpu_custom_call" | custom-call | tf_op jit(solution)/shard_map/add_rows/pallas_call | solution.py:388
Async XLA Ops:
  0.0 86.5 %copy-start.4 = (f32[1024]{0:T(1024)S(1)}, f32[1024]{0:T(1024)}, u32[]{:S(2)}) copy-start(f32[1024]{0:T(1024)} %param.9) | copy-start | bytes 12292
  0.0 86.5 %copy-start.3 = (s32[1024]{0:T(1024)S(1)}, s32[1024]{0:T(1024)}, u32[]{:S(2)}) copy-start(s32[1024]{0:T(1024)} %param.8) | copy-start | bytes 12292
  86.5 2.2 %copy-start = (bf16[1024,2048]{1,0:T(8,128)(2,1)S(1)}, bf16[1024,2048]{1,0:T(8,128)(2,1)}, u32[]{:S(2)}) copy-start(bf16[1024,2048]{1,0:T(8,128)(2,1)} %tok.1) | copy-start | bytes 12582916
  88.7 1.2 %copy-start.1 = (bf16[256,2048]{1,0:T(8,128)(2,1)S(1)}, bf16[256,2048]{1,0:T(8,128)(2,1)}, u32[]{:S(2)}) copy-start(bf16[256,2048]{1,0:T(8,128)(2,1)} %get-tuple-element.8.blk) | copy-start | bytes 3145732
  90.0 1.0 %copy-start.2 = (bf16[256,1024]{1,0:T(8,128)(2,1)S(1)}, bf16[256,1024]{1,0:T(8,128)(2,1)}, u32[]{:S(2)}) copy-start(bf16[256,1024]{1,0:T(8,128)(2,1)} %get-tuple-element.7.oh) | copy-start | bytes 1572868

commit v2 on v1

--- a/solution.py
+++ b/solution.py
@@ -18,11 +18,12 @@
 
 
 class Ring:
-    def __init__(self, geo, sems, region_in, region_y=None):
+    def __init__(self, geo, sems, region_in, paired=True, causal=False):
         self.g = geo
         self.sems = sems
         self.region_in = region_in
-        self.region_y = region_y
+        self.region_y = region_in if paired else None
+        self.causal = causal
         self.sends = []
         a_count, b_count = geo["A"], geo["B"]
         self.order = [(k, 0) for k in range(1, a_count)]
@@ -45,13 +46,28 @@
             device_id_type=MESH,
         )
 
-    def send(self, *args):
+    def send(self, *args, when=None):
         made = self.copy(*args)
-        made.start()
-        self.sends.append(made)
-
-    def arrive(self, kind, index, ref):
-        self.copy(kind, index, ref, self.g["dp"], self.g["z_next"]).wait_recv()
+        self.guard(when, made.start)
+        self.sends.append((when, made))
+
+    def guard(self, when, act):
+        if when is None:
+            act()
+        else:
+            pl.when(when)(act)
+
+    def fast_needed(self, k, b):
+        g = self.g
+        if not self.causal:
+            return None
+        here = g["a"] >= k
+        if g["B"] == 2 and k == 0:
+            return b == 1
+        return here
+
+    def arrive(self, kind, index, ref, when=None):
+        self.guard(when, self.copy(kind, index, ref, self.g["dp"], self.g["z_next"]).wait_recv)
 
     def mine(self, s):
         return self.region_in(s, self.g["y"], self.g["c"])
@@ -68,21 +84,27 @@
     def slow(self, k):
         g = self.g
         s = self.piece(k, 0)
+        came = (g["a"] >= k) if self.causal else None
+        goes = jnp.logical_and(g["a"] >= k, g["a"] < g["A"] - 1) if self.causal else None
         if k > 0:
-            self.arrive("z", k - 1, self.mine(s))
+            self.arrive("z", k - 1, self.mine(s), when=came)
         if k < g["A"] - 1:
-            self.send("z", k, self.mine(s), g["dp"], g["z_next"])
+            self.send("z", k, self.mine(s), g["dp"], g["z_next"], when=goes)
         if g["B"] > 1:
-            self.send("x", k * (g["B"] - 1), self.mine(s), g["dp"], g["x_next"])
+            there = lax.rem(g["b"] + 1, g["B"])
+            self.send(
+                "x", k * (g["B"] - 1), self.mine(s), g["dp"], g["x_next"], when=self.fast_needed(k, there)
+            )
         if k > 0:
             self.fan(k, 0)
 
     def fast(self, k, j):
         g = self.g
         s = self.piece(k, j)
-        self.arrive("x", k * (g["B"] - 1) + j - 1, self.mine(s))
+        need = self.fast_needed(k, g["b"])
+        self.arrive("x", k * (g["B"] - 1) + j - 1, self.mine(s), when=need)
         if j < g["B"] - 1:
-            self.send("x", k * (g["B"] - 1) + j, self.mine(s), g["dp"], g["x_next"])
+            self.send("x", k * (g["B"] - 1) + j, self.mine(s), g["dp"], g["x_next"], when=need)
         self.fan(k, j)
 
     def relay(self):
@@ -100,14 +122,14 @@
             self.arrive("d", len(self.order) + index, self.region_y(s, 1 - g["y"], 1 - g["c"]))
 
     def finish(self):
-        for made in self.sends:
-            made.wait_send()
+        for when, made in self.sends:
+            self.guard(when, made.wait_send)
 
 
 def main_kernel(
     A, B, tok, ch, wq, wk, wv, wo, blk, oh_out,
     tok_v, wbuf, obuf, kvbuf, normed, qs, acc, m_s, l_s, att, lsem,
-    wz, wx, wy, wd, oz, ox, oy, od, kz, kx,
+    ez, ex, ey, ed, qz, qx, qy, qd, oz, ox, oy, od, kz, kx,
 ):
     n = A * B
     dp = lax.axis_index("dp")
@@ -152,38 +174,31 @@
         pl.semaphore_signal(barrier, inc=1, device_id=who, device_id_type=MESH)
     pl.semaphore_wait(barrier, len(greet))
 
-    third = all_cols // 6
-
     def w_region(s, start, size):
         return wbuf.at[
             pl.ds(pl.multiple_of(s * k_rows, k_rows), k_rows),
             pl.ds(pl.multiple_of(start, 128), size),
         ]
 
-    o_half = o_rows // 2
-    o_y = o_half * 3 // 8 // 16 * 16
-    o_in = o_half - o_y
-
-    def o_region(s, start, size):
-        return obuf.at[s, pl.ds(pl.multiple_of(start, 16), size), :]
-
-    ring_w = Ring(
-        geo,
-        {"z": wz, "x": wx, "y": wy, "d": wd},
-        lambda s, y, c: w_region(s, c * (3 * third) + y * third, 2 * third),
-        lambda s, y, c: w_region(s, c * (3 * third) + y * (2 * third), third),
-    )
-    ring_o = Ring(
-        geo,
-        {"z": oz, "x": ox, "y": oy, "d": od},
-        lambda s, y, c: o_region(s, c * o_half + y * o_y, o_in),
-        lambda s, y, c: o_region(s, c * o_half + y * o_in, o_y),
-    )
-    ring_k = Ring(geo, {"z": kz, "x": kx}, lambda s, y, c: kvbuf.at[s])
-
-    for made in local[:3]:
-        made.wait()
-    ring_w.slow(0)
+    def quarters(first, size):
+        part = size // 4
+        return lambda s, y, c: w_region(s, first + (2 * c + y) * part, part)
+
+    o_part = o_rows // 4
+
+    def o_region(s, y, c):
+        return obuf.at[s, pl.ds(pl.multiple_of((2 * c + y) * o_part, o_part), o_part), :]
+
+    ring_e = Ring(geo, {"z": ez, "x": ex, "y": ey, "d": ed}, quarters(q_cols, 2 * e_cols))
+    ring_q = Ring(geo, {"z": qz, "x": qx, "y": qy, "d": qd}, quarters(0, q_cols))
+    ring_o = Ring(geo, {"z": oz, "x": ox, "y": oy, "d": od}, o_region)
+    ring_k = Ring(geo, {"z": kz, "x": kx}, lambda s, y, c: kvbuf.at[s], paired=False, causal=True)
+
+    local[1].wait()
+    local[2].wait()
+    ring_e.slow(0)
+    local[0].wait()
+    ring_q.slow(0)
 
     base = seq * t_rows
     picks = ch[...]
@@ -209,15 +224,16 @@
         normed[:, cols] = (normed[:, cols].astype(F32) * scale).astype(BF16)
 
     for k in range(1, A):
-        ring_w.slow(k)
-        for j in range(1, B):
-            ring_w.fast(k - 1, j)
+        for ring in (ring_e, ring_q):
+            ring.slow(k)
+            for j in range(1, B):
+                ring.fast(k - 1, j)
     for j in range(1, B):
-        ring_w.fast(A - 1, j)
+        ring_e.fast(A - 1, j)
     local[3].wait()
     ring_o.slow(0)
-    ring_w.relay()
-    ring_w.gather_core()
+    ring_e.relay()
+    ring_e.gather_core()
 
     kv_cols = 2 * e_cols
     for i in range(kv_cols // 256):
@@ -226,6 +242,10 @@
         )
         kvbuf[seq, :, i * 256 : (i + 1) * 256] = part.astype(BF16)
     ring_k.slow(0)
+    for j in range(1, B):
+        ring_q.fast(A - 1, j)
+    ring_q.relay()
+    ring_q.gather_core()
     group = HEADS // KV_HEADS
     for i in range(q_cols // 256):
         part = jnp.dot(normed[...], wbuf[:, i * 256 : (i + 1) * 256], preferred_element_type=F32)
@@ -309,7 +329,8 @@
         blk[:, s * o_cols : (s + 1) * o_cols] = jnp.dot(
             att[...], obuf[s], preferred_element_type=F32
         ).astype(BF16)
-    ring_w.finish()
+    ring_e.finish()
+    ring_q.finish()
     ring_k.finish()
     ring_o.finish()
 
@@ -346,7 +367,7 @@
         return (dma((count,)), dma((count,)))
 
     sems = []
-    for _ in range(2):
+    for _ in range(3):
         sems += [pair(A - 1), pair(steps_x), pair(n - 1), pair(2 * (n - 1))]
     sems += [pair(A - 1), pair(steps_x)]
     flat = [x for two in sems for x in two]
@@ -397,7 +418,7 @@
             pl.BlockSpec((MOST_OWN, width), lambda i: (0, 0)),
         ],
         out_specs=pl.BlockSpec((tile, width), lambda i: (i, 0)),
-        compiler_params=pltpu.CompilerParams(vmem_limit_bytes=32 * 1024 * 1024),
+        compiler_params=pltpu.CompilerParams(vmem_limit_bytes=62 * 1024 * 1024),
         name="add_rows",
     )(tokens, picks, gate_row, oh, blk)
 

time: 96.3 us -> 96.9 us (level); the launches traced: 96 us -> 95.5 us
  local copies, waits for them, and re-layouts: 4.46 us -> 0 us
  Pallas kernels: 91.5 us -> 95.5 us
    unnamed x10 -> x0, local copies, waits for them, and re-layouts: 4.46 us -> none
    pallas_call x1, Pallas kernels: 5.01 us -> 8.04 us  [per_device(): pl.pallas_call(functools.partial(add_kernel, tile), grid=(t_rows // tile,...]
    pallas_call x1, Pallas kernels: 86.5 us -> 87.5 us  [per_device(): pl.pallas_call(body, out_shape=(jax.ShapeDtypeStruct((MOST_OWN, width), B...]
where the time goes in v2:
time: 96.9 us; the launch traced here: 95.5 us
  Pallas kernels  95.5 us (99%)
    pallas_call x1, Pallas kernels, per_device(): pl.pallas_call(body, out_shape=(jax.ShapeDtypeStruct((MOST_OWN, width), B...  87.5 us
    pallas_call x1, Pallas kernels, per_device(): pl.pallas_call(functools.partial(add_kernel, tile), grid=(t_rows // tile,...  8.04 us

profile of v2, /device:TPU:28, one launch (start us, length us, event | category | flops | bytes accessed | tf_op | source)
XLA Modules:
  0.0 95.5 jit_solution(17190335436505312309)
XLA Ops:
  0.0 87.5 %gather_attend.1 = (bf16[256,2048]{1,0:T(8,128)(2,1)}, bf16[256,1024]{1,0:T(8,128)(2,1)}) custom-call(bf16[1024,2048]{1,0:T(8,128)(2,1)} %tok.1, s32[1,1024]{1,0:T(1,128)} %bitcast.2, bf16[256,1024]{1,0:T(8,128)(2,1)} %refs_2_.1, bf16[256,256]{1,0:T(8,128)(2,1)} %refs_3_.1, bf16[256,256]{1,0:T(8,128)(2,1)} %refs_4_.1, bf16[1024,256]{1,0:T(8,128)(2,1)} %refs_5_.1), custom_call_target="tpu_custom_call" | custom-call | tf_op jit(solution)/shard_map/gather_attend/pallas_call | solution.py:380
  87.5 8.0 %add_rows.1 = bf16[1024,2048]{1,0:T(8,128)(2,1)} custom-call(bf16[1024,2048]{1,0:T(8,128)(2,1)} %tok.1, s32[1,1024]{1,0:T(1,128)} %bitcast.3, f32[1,1024]{1,0:T(1,128)} %bitcast.4, bf16[256,1024]{1,0:T(8,128)(2,1)} %get-tuple-element.7.oh, bf16[256,2048]{1,0:T(8,128)(2,1)} %get-tuple-element.8.blk), custom_call_target="tpu_custom_call" | custom-call | tf_op jit(solution)/shard_map/add_rows/pallas_call | solution.py:409
